TPU v7x, 32 devices: a whole 2x2x4 slice. The times are simulated.
32 devices in a mesh: gene: 8 (over z, x), cell: 4 (over y, core).
Axes of the slice: x: 2, y: 2, z: 4, core: 2. Of those that a mesh axis runs over, the one named last changes fastest.
Arguments:
- pool_counts: bfloat16 [20480, 16384], P('gene', 'cell'), may hold values from 0 to 6.5
- cell_picks: int32 [7, 4096], P(None, 'cell'), may hold values from 0 to 16383, as said below
- loadings_init: float32 [64, 20480], P(None, 'gene'), may hold values from -0.0390625 to 0.0390625
Outputs:
- scaled_loadings: float32 [64, 20480], P(None, 'gene')
Inputs may be any that keep to these rules, and one draw needn't show every extreme that they name: `cell_picks`: column b of every row names a pool cell in [(b // 1024) * 4096, (b // 1024 + 1) * 4096); no cell is named twice in one row.
All inputs are finite; a program needn't handle non-finite values.
Results may differ from a plain program's by a relative error of at most 0.018.
Values may be sent and summed in bfloat16 or wider, within the bound.
A program may use at most 128 MiB of HBM per device.

v0:
```python
import math
import jax
import jax.numpy as jnp
from jax import lax
from jax.sharding import PartitionSpec as P

STEPS = 7
step_rate = 1.0


def transposed_product(left, right):
    return lax.dot_general(
        left, right, (((1,), (1,)), ((), ())), preferred_element_type=jnp.float32
    )


def shards(pool_counts, cell_picks, loadings_init):
    loadings = loadings_init
    local_pool = pool_counts.shape[1]
    group = lax.axis_index("cell")
    batch_total = cell_picks.shape[1] * lax.axis_size("cell")
    gene_total = loadings.shape[1] * lax.axis_size("gene")
    for step_index in range(STEPS):
        chosen = cell_picks[step_index] - group * local_pool
        gathered = jnp.take(pool_counts, chosen, axis=1)
        weights_low = loadings.astype(jnp.bfloat16)
        product = jnp.dot(weights_low, gathered, preferred_element_type=jnp.float32)
        local_sums = jnp.sum(gathered, axis=1, dtype=jnp.float32)
        batch_means = lax.psum(local_sums, "cell") / batch_total
        shift = jnp.dot(
            weights_low.astype(jnp.float32), batch_means, precision=lax.Precision.HIGHEST
        )
        partial_value = product - shift[:, None]
        scores = lax.psum(partial_value, "gene")
        scores_low = scores.astype(jnp.bfloat16)
        raw_update = transposed_product(scores_low, gathered)
        row_totals = jnp.sum(scores_low, axis=1, dtype=jnp.float32)
        local_update = (raw_update - row_totals[:, None] * batch_means[None, :]) / batch_total
        update = lax.psum(local_update.astype(jnp.bfloat16), "cell").astype(jnp.float32)
        stepped = loadings + step_rate * update
        gram_part = jnp.dot(stepped, stepped.T, precision=lax.Precision.HIGHEST)
        gram_matrix = lax.psum(gram_part, "gene")
        factor = jnp.linalg.cholesky(gram_matrix)
        loadings = lax.linalg.triangular_solve(factor, stepped, left_side=True, lower=True)
    return loadings * math.sqrt(gene_total)


def solution(mesh):
    placed = (P("gene", "cell"), P(None, "cell"), P(None, "gene"))
    return jax.shard_map(
        shards, mesh=mesh, in_specs=placed, out_specs=P(None, "gene"), check_vma=False
    )
```

profile of v0, /device:TPU:0, one launch (start us, length us, event | category | flops | bytes accessed | tf_op | source)
XLA Modules:
  0.0 1143.4 jit_solution(7488319310404820462)
XLA Ops:
  7.8 25.9 %copy.4 = bf16[2560,4096]{0,1:T(8,128)(2,1)} copy(bf16[2560,4096]{1,0:T(8,128)(2,1)} %param.8) | data formatting | bytes 41943040 | tf_op args[0]
  33.7 20.2 %gather_fusion.6 = bf16[1024,2560]{1,0:T(8,128)(2,1)} fusion(bf16[2560,4096]{0,1:T(8,128)(2,1)} %copy.4, s32[1024]{0:T(1024)S(1)} %fusion.188), kind=kCustom, calls=%fused_computation.6.clone | custom fusion | bytes 10489856 | tf_op jit(solution)/shard_map/jit(_take)/gather | solution.py:25
  53.8 20.1 %gather_fusion.5 = bf16[1024,2560]{1,0:T(8,128)(2,1)} fusion(bf16[2560,4096]{0,1:T(8,128)(2,1)} %copy.4, s32[1024]{0:T(1024)S(1)} %fusion.187), kind=kCustom, calls=%fused_computation.5.clone | custom fusion | bytes 10489856 | tf_op jit(solution)/shard_map/jit(_take)/gather | solution.py:25
  73.9 20.5 %gather_fusion.4 = bf16[1024,2560]{1,0:T(8,128)(2,1)} fusion(bf16[2560,4096]{0,1:T(8,128)(2,1)} %copy.4, s32[1024]{0:T(1024)S(1)} %fusion.186), kind=kCustom, calls=%fused_computation.4.clone | custom fusion | bytes 10489856 | tf_op jit(solution)/shard_map/jit(_take)/gather | solution.py:25
  94.5 20.1 %gather_fusion.3 = bf16[1024,2560]{1,0:T(8,128)(2,1)} fusion(bf16[2560,4096]{0,1:T(8,128)(2,1)} %copy.4, s32[1024]{0:T(1024)S(1)} %fusion.185), kind=kCustom, calls=%fused_computation.3.clone | custom fusion | bytes 10489856 | tf_op jit(solution)/shard_map/jit(_take)/gather | solution.py:25
  114.6 20.2 %gather_fusion.2 = bf16[1024,2560]{1,0:T(8,128)(2,1)} fusion(bf16[2560,4096]{0,1:T(8,128)(2,1)} %copy.4, s32[1024]{0:T(1024)S(1)} %fusion.184), kind=kCustom, calls=%fused_computation.2.clone | custom fusion | bytes 10489856 | tf_op jit(solution)/shard_map/jit(_take)/gather | solution.py:25
  134.8 20.1 %gather_fusion.1 = bf16[1024,2560]{1,0:T(8,128)(2,1)} fusion(bf16[2560,4096]{0,1:T(8,128)(2,1)} %copy.4, s32[1024]{0:T(1024)S(1)} %fusion.183), kind=kCustom, calls=%fused_computation.1.clone | custom fusion | bytes 10489856 | tf_op jit(solution)/shard_map/jit(_take)/gather | solution.py:25
  154.9 20.1 %gather_fusion = bf16[1024,2560]{1,0:T(8,128)(2,1)} fusion(bf16[2560,4096]{0,1:T(8,128)(2,1)} %copy.4, s32[1024]{0:T(1024)S(1)} %fusion.182), kind=kCustom, calls=%fused_computation.clone | custom fusion | bytes 10489856 | tf_op jit(solution)/shard_map/jit(_take)/gather | solution.py:25
  179.3 7.3 convert_reduce_fusion
  186.6 5.4 convert_reduce_fusion.2
  195.6 33.5 %all-reduce.31.cloned.1.call-done = (f32[2560]{0:T(1024)}, f32[2560]{0:T(1024)}, f32[2560]{0:T(1024)}, f32[2560]{0:T(1024)}, f32[2560]{0:T(1024)}, /*index=5*/f32[2560]{0:T(1024)}, f32[2560]{0:T(1024)}) async-done(((f32[2560]{0:T(1024)}, f32[2560]{0:T(1024)}, f32[2560]{0:T(1024)}, f32[2560]{0:T(1024)}, f32[2560]{0:T(1024)}, /*index=5*/f32[2560]{0:T(1024)}, f32[2560]{0:T(1024)}), (f32[2560]{0:T(1024)}, ...) | async-done | bytes 71696 | tf_op jit(solution)/shard_map/psum | solution.py:29
  234.5 40.8 %all-reduce.32 = bf16[64,1024]{1,0:T(8,128)(2,1)S(1)} all-reduce(f32[64,1024]{1,0:T(8,128)S(1)} %fusion.94), channel_id=1, replica_groups=mesh['gene'=8,'cell'=4] {'gene'}, use_global_device_ids=true, to_apply=%region_2.4 | all-reduce | flops 65536 | bytes 393216 | tf_op jit(solution)/shard_map/psum | solution.py:34
  279.9 30.0 %all-reduce.17.cloned.1.call-done = bf16[64,2560]{1,0:T(8,128)(2,1)} async-done(((bf16[64,2560]{1,0:T(8,128)(2,1)}), bf16[64,2560]{1,0:T(8,128)(2,1)}) %all-reduce.17.cloned.1.call-update) | async-done | bytes 327696 | tf_op jit(solution)/shard_map/psum | solution.py:39
  311.8 37.1 %psum.199 = f32[64,64]{0,1:T(8,128)S(1)} all-reduce(f32[64,64]{0,1:T(8,128)S(1)} %fusion.116), channel_id=1, replica_groups=mesh['gene'=8,'cell'=4] {'gene'}, use_global_device_ids=true, to_apply=%region_5.7 | all-reduce | flops 4096 | bytes 32768 | tf_op jit(solution)/shard_map/psum | solution.py:42
  348.9 5.8 cholesky.119
  356.1 4.9 custom-call.11
  367.4 36.0 %all-reduce.33 = bf16[64,1024]{1,0:T(8,128)(2,1)S(1)} all-reduce(f32[64,1024]{1,0:T(8,128)S(1)} %fusion.97), channel_id=1, replica_groups=mesh['gene'=8,'cell'=4] {'gene'}, use_global_device_ids=true, to_apply=%region_10.0 | all-reduce | flops 65536 | bytes 393216 | tf_op jit(solution)/shard_map/psum | solution.py:34
  408.1 30.5 %all-reduce.19.cloned.1.call-done = bf16[64,2560]{1,0:T(8,128)(2,1)} async-done(((bf16[64,2560]{1,0:T(8,128)(2,1)}), bf16[64,2560]{1,0:T(8,128)(2,1)}) %all-reduce.19.cloned.1.call-update) | async-done | bytes 327696 | tf_op jit(solution)/shard_map/psum | solution.py:39
  440.4 37.6 %psum.203 = f32[64,64]{0,1:T(8,128)S(1)} all-reduce(f32[64,64]{0,1:T(8,128)S(1)} %fusion.118), channel_id=1, replica_groups=mesh['gene'=8,'cell'=4] {'gene'}, use_global_device_ids=true, to_apply=%region_13.0 | all-reduce | flops 4096 | bytes 32768 | tf_op jit(solution)/shard_map/psum | solution.py:42
  478.1 5.8 cholesky.130
  485.3 4.9 custom-call.12
  496.6 36.0 %all-reduce.34 = bf16[64,1024]{1,0:T(8,128)(2,1)S(1)} all-reduce(f32[64,1024]{1,0:T(8,128)S(1)} %fusion.100), channel_id=1, replica_groups=mesh['gene'=8,'cell'=4] {'gene'}, use_global_device_ids=true, to_apply=%region_16.0 | all-reduce | flops 65536 | bytes 393216 | tf_op jit(solution)/shard_map/psum | solution.py:34
  537.2 30.6 %all-reduce.21.cloned.1.call-done = bf16[64,2560]{1,0:T(8,128)(2,1)} async-done(((bf16[64,2560]{1,0:T(8,128)(2,1)}), bf16[64,2560]{1,0:T(8,128)(2,1)}) %all-reduce.21.cloned.1.call-update) | async-done | bytes 327696 | tf_op jit(solution)/shard_map/psum | solution.py:39
  569.7 37.1 %psum.207 = f32[64,64]{0,1:T(8,128)S(1)} all-reduce(f32[64,64]{0,1:T(8,128)S(1)} %fusion.120), channel_id=1, replica_groups=mesh['gene'=8,'cell'=4] {'gene'}, use_global_device_ids=true, to_apply=%region_19.0 | all-reduce | flops 4096 | bytes 32768 | tf_op jit(solution)/shard_map/psum | solution.py:42
  606.9 5.8 cholesky.141
  614.0 4.9 custom-call.13
  625.3 36.0 %all-reduce.35 = bf16[64,1024]{1,0:T(8,128)(2,1)S(1)} all-reduce(f32[64,1024]{1,0:T(8,128)S(1)} %fusion.103), channel_id=1, replica_groups=mesh['gene'=8,'cell'=4] {'gene'}, use_global_device_ids=true, to_apply=%region_22.0 | all-reduce | flops 65536 | bytes 393216 | tf_op jit(solution)/shard_map/psum | solution.py:34
  661.5 4.4 fusion.79
  666.2 30.4 %all-reduce.23.cloned.1.call-done = bf16[64,2560]{1,0:T(8,128)(2,1)} async-done(((bf16[64,2560]{1,0:T(8,128)(2,1)}), bf16[64,2560]{1,0:T(8,128)(2,1)}) %all-reduce.23.cloned.1.call-update) | async-done | bytes 327696 | tf_op jit(solution)/shard_map/psum | solution.py:39
  698.4 37.1 %psum.211 = f32[64,64]{0,1:T(8,128)S(1)} all-reduce(f32[64,64]{0,1:T(8,128)S(1)} %fusion.122), channel_id=1, replica_groups=mesh['gene'=8,'cell'=4] {'gene'}, use_global_device_ids=true, to_apply=%region_25.0 | all-reduce | flops 4096 | bytes 32768 | tf_op jit(solution)/shard_map/psum | solution.py:42
  735.6 5.8 cholesky.152
  742.8 4.9 custom-call.14
  754.0 36.0 %all-reduce.36 = bf16[64,1024]{1,0:T(8,128)(2,1)S(1)} all-reduce(f32[64,1024]{1,0:T(8,128)S(1)} %fusion.106), channel_id=1, replica_groups=mesh['gene'=8,'cell'=4] {'gene'}, use_global_device_ids=true, to_apply=%region_28.0 | all-reduce | flops 65536 | bytes 393216 | tf_op jit(solution)/shard_map/psum | solution.py:34
  794.6 30.7 %all-reduce.25.cloned.1.call-done = bf16[64,2560]{1,0:T(8,128)(2,1)} async-done(((bf16[64,2560]{1,0:T(8,128)(2,1)}), bf16[64,2560]{1,0:T(8,128)(2,1)}) %all-reduce.25.cloned.1.call-update) | async-done | bytes 327696 | tf_op jit(solution)/shard_map/psum | solution.py:39
  827.1 37.1 %psum.215 = f32[64,64]{0,1:T(8,128)S(1)} all-reduce(f32[64,64]{0,1:T(8,128)S(1)} %fusion.124), channel_id=1, replica_groups=mesh['gene'=8,'cell'=4] {'gene'}, use_global_device_ids=true, to_apply=%region_31.0 | all-reduce | flops 4096 | bytes 32768 | tf_op jit(solution)/shard_map/psum | solution.py:42
  864.3 5.8 cholesky.163
  871.5 4.9 custom-call.15
  882.8 36.2 %all-reduce.37 = bf16[64,1024]{1,0:T(8,128)(2,1)S(1)} all-reduce(f32[64,1024]{1,0:T(8,128)S(1)} %fusion.109), channel_id=1, replica_groups=mesh['gene'=8,'cell'=4] {'gene'}, use_global_device_ids=true, to_apply=%region_34.0 | all-reduce | flops 65536 | bytes 393216 | tf_op jit(solution)/shard_map/psum | solution.py:34
  923.6 30.5 %all-reduce.27.cloned.1.call-done = bf16[64,2560]{1,0:T(8,128)(2,1)} async-done(((bf16[64,2560]{1,0:T(8,128)(2,1)}), bf16[64,2560]{1,0:T(8,128)(2,1)}) %all-reduce.27.cloned.1.call-update) | async-done | bytes 327696 | tf_op jit(solution)/shard_map/psum | solution.py:39
  956.0 37.1 %psum.219 = f32[64,64]{0,1:T(8,128)S(1)} all-reduce(f32[64,64]{0,1:T(8,128)S(1)} %fusion.126), channel_id=1, replica_groups=mesh['gene'=8,'cell'=4] {'gene'}, use_global_device_ids=true, to_apply=%region_37.0 | all-reduce | flops 4096 | bytes 32768 | tf_op jit(solution)/shard_map/psum | solution.py:42
  993.2 5.8 cholesky.174
  1000.3 4.9 custom-call.16
  1011.6 35.9 %all-reduce.38 = bf16[64,1024]{1,0:T(8,128)(2,1)S(1)} all-reduce(f32[64,1024]{1,0:T(8,128)S(1)} %fusion.112), channel_id=1, replica_groups=mesh['gene'=8,'cell'=4] {'gene'}, use_global_device_ids=true, to_apply=%region_40.0 | all-reduce | flops 65536 | bytes 393216 | tf_op jit(solution)/shard_map/psum | solution.py:34
  1047.7 4.4 fusion.88
  1052.1 30.7 %all-reduce.29.cloned.1.call-done = bf16[64,2560]{1,0:T(8,128)(2,1)} async-done(((bf16[64,2560]{1,0:T(8,128)(2,1)}), bf16[64,2560]{1,0:T(8,128)(2,1)}) %all-reduce.29.cloned.1.call-update) | async-done | bytes 327696 | tf_op jit(solution)/shard_map/psum | solution.py:39
  1084.5 37.1 %psum.223 = f32[64,64]{0,1:T(8,128)S(1)} all-reduce(f32[64,64]{0,1:T(8,128)S(1)} %fusion.127), channel_id=1, replica_groups=mesh['gene'=8,'cell'=4] {'gene'}, use_global_device_ids=true, to_apply=%region_43.47 | all-reduce | flops 4096 | bytes 32768 | tf_op jit(solution)/shard_map/psum | solution.py:42
  1121.7 5.8 cholesky.185
  1128.9 4.9 custom-call.17
  (151 shorter events, 101.1 us)
Async XLA Ops:
  6.5 222.6 %all-reduce.31.cloned.1.call-start = ((), (), s32[]{:S(2)}) async-start(), calls=%async_computation.7 | async-start | bytes 172032 | tf_op jit(solution)/shard_map/psum | solution.py:29
  175.0 11.6 %slice-start = ((s8[5242880]{0:T(1024)(128)(4,1)}), s8[1048576]{0:T(1024)(128)(4,1)S(1)}, s32[]{:S(2)}) async-start(s8[5242880]{0:T(1024)(128)(4,1)} %bitcast.200), calls=%async_computation.8 | async-start | bytes 2097152
  179.3 7.3 slice-start.1
  179.3 12.7 %slice-start.2 = ((s8[5242880]{0:T(1024)(128)(4,1)}), s8[4194304]{0:T(1024)(128)(4,1)S(1)}, s32[]{:S(2)}) async-start(s8[5242880]{0:T(1024)(128)(4,1)} %bitcast.202), calls=%async_computation.10 | async-start | bytes 8388608
  179.3 12.7 %slice-start.4 = ((s8[5242880]{0:T(1024)(128)(4,1)}), s8[4194304]{0:T(1024)(128)(4,1)S(1)}, s32[]{:S(2)}) async-start(s8[5242880]{0:T(1024)(128)(4,1)} %bitcast.204), calls=%async_computation.12 | async-start | bytes 8388608
  186.6 5.4 slice-start.3
  186.6 5.4 slice-start.5
  192.0 37.8 %copy-start = (f32[64,2560]{1,0:T(8,128)S(1)}, f32[64,2560]{1,0:T(8,128)}, u32[]{:S(2)}) copy-start(f32[64,2560]{1,0:T(8,128)} %param.10) | copy-start | bytes 1966084
  195.6 114.4 %all-reduce.17.cloned.1.call-start = ((), (), s32[]{:S(2)}) async-start(), calls=%async_computation | async-start | bytes 655360 | tf_op jit(solution)/shard_map/psum | solution.py:39
  234.5 45.4 %copy-start.6 = (f32[2560]{0:T(1024)S(1)}, f32[2560]{0:T(1024)}, u32[]{:S(2)}) copy-start(f32[2560]{0:T(1024)} %get-tuple-element.8) | copy-start | bytes 30724
  279.8 158.7 %all-reduce.19.cloned.1.call-start = ((), (), s32[]{:S(2)}) async-start(), calls=%async_computation.1 | async-start | bytes 655360 | tf_op jit(solution)/shard_map/psum | solution.py:39
  367.4 40.6 %copy-start.5 = (f32[2560]{0:T(1024)S(1)}, f32[2560]{0:T(1024)}, u32[]{:S(2)}) copy-start(f32[2560]{0:T(1024)} %get-tuple-element.10) | copy-start | bytes 30724
  408.0 159.9 %all-reduce.21.cloned.1.call-start = ((), (), s32[]{:S(2)}) async-start(), calls=%async_computation.2 | async-start | bytes 655360 | tf_op jit(solution)/shard_map/psum | solution.py:39
  496.6 40.6 %copy-start.4 = (f32[2560]{0:T(1024)S(1)}, f32[2560]{0:T(1024)}, u32[]{:S(2)}) copy-start(f32[2560]{0:T(1024)} %get-tuple-element.11) | copy-start | bytes 30724
  537.1 159.4 %all-reduce.23.cloned.1.call-start = ((), (), s32[]{:S(2)}) async-start(), calls=%async_computation.3 | async-start | bytes 655360 | tf_op jit(solution)/shard_map/psum | solution.py:39
  625.3 40.8 %copy-start.3 = (f32[2560]{0:T(1024)S(1)}, f32[2560]{0:T(1024)}, u32[]{:S(2)}) copy-start(f32[2560]{0:T(1024)} %get-tuple-element.12) | copy-start | bytes 30724
  665.9 159.4 %all-reduce.25.cloned.1.call-start = ((), (), s32[]{:S(2)}) async-start(), calls=%async_computation.4 | async-start | bytes 655360 | tf_op jit(solution)/shard_map/psum | solution.py:39
  754.0 40.6 %copy-start.2 = (f32[2560]{0:T(1024)S(1)}, f32[2560]{0:T(1024)}, u32[]{:S(2)}) copy-start(f32[2560]{0:T(1024)} %get-tuple-element.13) | copy-start | bytes 30724
  794.5 159.6 %all-reduce.27.cloned.1.call-start = ((), (), s32[]{:S(2)}) async-start(), calls=%async_computation.5 | async-start | bytes 655360 | tf_op jit(solution)/shard_map/psum | solution.py:39
  882.8 40.9 %copy-start.1 = (f32[2560]{0:T(1024)S(1)}, f32[2560]{0:T(1024)}, u32[]{:S(2)}) copy-start(f32[2560]{0:T(1024)} %get-tuple-element.14) | copy-start | bytes 30724
  923.5 159.2 %all-reduce.29.cloned.1.call-start = ((), (), s32[]{:S(2)}) async-start(), calls=%async_computation.6 | async-start | bytes 655360 | tf_op jit(solution)/shard_map/psum | solution.py:39
Sparse Core Ops, SparseCore 0:
  195.7 33.3 all-reduce.30
  280.0 29.9 all-reduce.16
  408.1 30.4 all-reduce.18
  537.3 30.5 all-reduce.20
  666.0 30.5 all-reduce.22
  794.7 30.5 all-reduce.24
  923.7 30.4 all-reduce.26
  1052.2 30.4 all-reduce.28
where the time goes:
time: 1150 us; the launch traced here: 1140 us
  blocking collectives  517 us (45%)
  waiting for transfers between devices  247 us (21%)
  local copies, waits for them, and re-layouts  168 us (15%)
  other arithmetic  108 us (9%)
  matrix products  88.8 us (8%)
  between operations  14.4 us (1%)
    psum x7, blocking collectives, shards(): gram_matrix = lax.psum(gram_part, 'gene')  260 us
    psum x7, blocking collectives, shards(): scores = lax.psum(partial_value, 'gene')  257 us
    psum x7, waiting for transfers between devices, shards(): lax.psum(local_update.astype(jnp.bfloat16), 'cell').astype(jnp.float32)  213 us
    gather x7, local copies, waits for them, and re-layouts, shards(): gathered = jnp.take(pool_counts, chosen, axis=1)  141 us
    another operation x21, other arithmetic, shards(): factor = jnp.linalg.cholesky(gram_matrix)  45.6 us
    another operation x14, other arithmetic, shards(): lax.linalg.triangular_solve(factor, stepped, left_side=True, lower=True)  38.8 us
    psum x1, waiting for transfers between devices, shards(): batch_means = lax.psum(local_sums, 'cell') / batch_total  33.5 us
    dot_general x7, matrix products, transposed_product(): lax.dot_general(left, right, (((1,), (1,)), ((), ())), preferred_element_...  30.7 us
  transfers between devices with their start and end apart: 8, of which 8 were waited for; matrix products, arithmetic and copies ran while one was open for 0% of the time, Pallas kernels for 0%

commit v1 on v0

--- a/solution.py
+++ b/solution.py
@@ -31,7 +31,9 @@
             weights_low.astype(jnp.float32), batch_means, precision=lax.Precision.HIGHEST
         )
         partial_value = product - shift[:, None]
-        scores = lax.psum(partial_value, "gene")
+        scores = partial_value
+        for hop in (1, 2, 4):
+            scores = scores + lax.ppermute(scores, "gene", [(dev, dev ^ hop) for dev in range(8)])
         scores_low = scores.astype(jnp.bfloat16)
         raw_update = transposed_product(scores_low, gathered)
         row_totals = jnp.sum(scores_low, axis=1, dtype=jnp.float32)

time: 1150 us -> 1050 us (0.913)
  blocking collectives: 517 us -> 260 us
  waiting for transfers between devices: 247 us -> 406 us
  matrix products: 88.8 us -> 75.1 us
    psum x7 -> x0, blocking collectives: 257 us -> none  [shards(): scores = lax.psum(partial_value, 'gene')]
    ppermute x0 -> x21, waiting for transfers between devices: none -> 161 us  [shards(): lax.ppermute(scores, 'gene', [(dev, dev ^ hop) for dev in range(8)])]
    dot_general x7, matrix products: 30.7 us -> 16 us  [transposed_product(): lax.dot_general(left, right, (((1,), (1,)), ((), ())), preferred_element_...]
    unnamed x27 -> x51, local copies, waits for them, and re-layouts: 25.9 us -> 26 us
  transfers between devices with their start and end apart: 8 -> 29, of which waited for: 8 -> 29; matrix products, arithmetic and copies ran while one was open for 0% -> 0% of each run, Pallas kernels for 0% -> 0%
where the time goes in v1:
time: 1050 us; the launch traced here: 1040 us
  waiting for transfers between devices  406 us (39%)
  blocking collectives  260 us (25%)
  local copies, waits for them, and re-layouts  168 us (16%)
  other arithmetic  109 us (10%)
  matrix products  75.1 us (7%)
  between operations  14.9 us (1%)
    psum x7, blocking collectives, shards(): gram_matrix = lax.psum(gram_part, 'gene')  260 us
    psum x7, waiting for transfers between devices, shards(): lax.psum(local_update.astype(jnp.bfloat16), 'cell').astype(jnp.float32)  212 us
    ppermute x21, waiting for transfers between devices, shards(): lax.ppermute(scores, 'gene', [(dev, dev ^ hop) for dev in range(8)])  161 us
    gather x7, local copies, waits for them, and re-layouts, shards(): gathered = jnp.take(pool_counts, chosen, axis=1)  141 us
    another operation x21, other arithmetic, shards(): factor = jnp.linalg.cholesky(gram_matrix)  45.6 us
    another operation x14, other arithmetic, shards(): lax.linalg.triangular_solve(factor, stepped, left_side=True, lower=True)  38.8 us
    psum x1, waiting for transfers between devices, shards(): batch_means = lax.psum(local_sums, 'cell') / batch_total  33.5 us
    dot_general x7, matrix products, shards(): product = jnp.dot(weights_low, gathered, preferred_element_type=jnp.float32)  30.7 us
  transfers between devices with their start and end apart: 29, of which 29 were waited for; matrix products, arithmetic and copies ran while one was open for 0% of the time, Pallas kernels for 0%

profile of v1, /device:TPU:0, one launch (start us, length us, event | category | flops | bytes accessed | tf_op | source)
XLA Modules:
  0.0 1041.1 jit_solution(3187387344521798526)
XLA Ops:
  7.8 25.9 %copy.4 = bf16[2560,4096]{0,1:T(8,128)(2,1)} copy(bf16[2560,4096]{1,0:T(8,128)(2,1)} %param.8) | data formatting | bytes 41943040 | tf_op args[0]
  33.7 20.2 %gather_fusion.6 = bf16[1024,2560]{1,0:T(8,128)(2,1)} fusion(bf16[2560,4096]{0,1:T(8,128)(2,1)} %copy.4, s32[1024]{0:T(1024)S(1)} %fusion.181), kind=kCustom, calls=%fused_computation.6.clone | custom fusion | bytes 10489856 | tf_op jit(solution)/shard_map/jit(_take)/gather | solution.py:25
  53.8 20.1 %gather_fusion.5 = bf16[1024,2560]{1,0:T(8,128)(2,1)} fusion(bf16[2560,4096]{0,1:T(8,128)(2,1)} %copy.4, s32[1024]{0:T(1024)S(1)} %fusion.180), kind=kCustom, calls=%fused_computation.5.clone | custom fusion | bytes 10489856 | tf_op jit(solution)/shard_map/jit(_take)/gather | solution.py:25
  73.9 20.3 %gather_fusion.4 = bf16[1024,2560]{1,0:T(8,128)(2,1)} fusion(bf16[2560,4096]{0,1:T(8,128)(2,1)} %copy.4, s32[1024]{0:T(1024)S(1)} %fusion.179), kind=kCustom, calls=%fused_computation.4.clone | custom fusion | bytes 10489856 | tf_op jit(solution)/shard_map/jit(_take)/gather | solution.py:25
  94.2 20.1 %gather_fusion.3 = bf16[1024,2560]{1,0:T(8,128)(2,1)} fusion(bf16[2560,4096]{0,1:T(8,128)(2,1)} %copy.4, s32[1024]{0:T(1024)S(1)} %fusion.178), kind=kCustom, calls=%fused_computation.3.clone | custom fusion | bytes 10489856 | tf_op jit(solution)/shard_map/jit(_take)/gather | solution.py:25
  114.3 20.3 %gather_fusion.2 = bf16[1024,2560]{1,0:T(8,128)(2,1)} fusion(bf16[2560,4096]{0,1:T(8,128)(2,1)} %copy.4, s32[1024]{0:T(1024)S(1)} %fusion.177), kind=kCustom, calls=%fused_computation.2.clone | custom fusion | bytes 10489856 | tf_op jit(solution)/shard_map/jit(_take)/gather | solution.py:25
  134.6 20.1 %gather_fusion.1 = bf16[1024,2560]{1,0:T(8,128)(2,1)} fusion(bf16[2560,4096]{0,1:T(8,128)(2,1)} %copy.4, s32[1024]{0:T(1024)S(1)} %fusion.176), kind=kCustom, calls=%fused_computation.1.clone | custom fusion | bytes 10489856 | tf_op jit(solution)/shard_map/jit(_take)/gather | solution.py:25
  154.7 20.1 %gather_fusion = bf16[1024,2560]{1,0:T(8,128)(2,1)} fusion(bf16[2560,4096]{0,1:T(8,128)(2,1)} %copy.4, s32[1024]{0:T(1024)S(1)} %fusion.175), kind=kCustom, calls=%fused_computation.clone | custom fusion | bytes 10489856 | tf_op jit(solution)/shard_map/jit(_take)/gather | solution.py:25
  179.0 7.3 convert_reduce_fusion
  195.6 33.5 %all-reduce.24.cloned.1.call-done = (f32[2560]{0:T(1024)}, f32[2560]{0:T(1024)}, f32[2560]{0:T(1024)}, f32[2560]{0:T(1024)}, f32[2560]{0:T(1024)}, /*index=5*/f32[2560]{0:T(1024)}, f32[2560]{0:T(1024)}) async-done(((f32[2560]{0:T(1024)}, f32[2560]{0:T(1024)}, f32[2560]{0:T(1024)}, f32[2560]{0:T(1024)}, f32[2560]{0:T(1024)}, /*index=5*/f32[2560]{0:T(1024)}, f32[2560]{0:T(1024)}), (f32[2560]{0:T(1024)}, ...) | async-done | bytes 71696 | tf_op jit(solution)/shard_map/psum | solution.py:29
  236.4 6.8 collective-permute-done
  245.1 6.0 collective-permute-done.1
  253.8 10.7 %collective-permute-done.2 = f32[64,1024]{1,0:T(8,128)S(1)} collective-permute-done((f32[64,1024]{1,0:T(8,128)S(1)}, f32[64,1024]{1,0:T(8,128)S(1)}, u32[]{:S(2)}, u32[]{:S(2)}) %collective-permute-start.2) | collective-permute-done | bytes 262176 | tf_op jit(solution)/shard_map/ppermute | solution.py:36
  266.7 32.8 %all-reduce.10.cloned.1.call-done = bf16[64,2560]{1,0:T(8,128)(2,1)} async-done(((bf16[64,2560]{1,0:T(8,128)(2,1)}), bf16[64,2560]{1,0:T(8,128)(2,1)}) %all-reduce.10.cloned.1.call-update) | async-done | bytes 327696 | tf_op jit(solution)/shard_map/psum | solution.py:41
  301.4 37.1 %psum.149 = f32[64,64]{0,1:T(8,128)S(1)} all-reduce(f32[64,64]{0,1:T(8,128)S(1)} %fusion.116), channel_id=1, replica_groups=mesh['gene'=8,'cell'=4] {'gene'}, use_global_device_ids=true, to_apply=%region_4.6 | all-reduce | flops 4096 | bytes 32768 | tf_op jit(solution)/shard_map/psum | solution.py:44
  338.5 5.8 cholesky.119
  357.3 6.4 collective-permute-done.3
  363.8 7.5 collective-permute-done.4
  371.4 9.0 collective-permute-done.5
  382.7 29.8 %all-reduce.12.cloned.1.call-done = bf16[64,2560]{1,0:T(8,128)(2,1)} async-done(((bf16[64,2560]{1,0:T(8,128)(2,1)}), bf16[64,2560]{1,0:T(8,128)(2,1)}) %all-reduce.12.cloned.1.call-update) | async-done | bytes 327696 | tf_op jit(solution)/shard_map/psum | solution.py:41
  414.3 37.4 %psum.152 = f32[64,64]{0,1:T(8,128)S(1)} all-reduce(f32[64,64]{0,1:T(8,128)S(1)} %fusion.118), channel_id=1, replica_groups=mesh['gene'=8,'cell'=4] {'gene'}, use_global_device_ids=true, to_apply=%region_11.0 | all-reduce | flops 4096 | bytes 32768 | tf_op jit(solution)/shard_map/psum | solution.py:44
  451.8 5.8 cholesky.130
  470.5 6.4 collective-permute-done.6
  477.0 7.5 collective-permute-done.7
  484.7 9.0 collective-permute-done.8
  495.9 29.9 %all-reduce.14.cloned.1.call-done = bf16[64,2560]{1,0:T(8,128)(2,1)} async-done(((bf16[64,2560]{1,0:T(8,128)(2,1)}), bf16[64,2560]{1,0:T(8,128)(2,1)}) %all-reduce.14.cloned.1.call-update) | async-done | bytes 327696 | tf_op jit(solution)/shard_map/psum | solution.py:41
  527.6 37.2 %psum.155 = f32[64,64]{0,1:T(8,128)S(1)} all-reduce(f32[64,64]{0,1:T(8,128)S(1)} %fusion.120), channel_id=1, replica_groups=mesh['gene'=8,'cell'=4] {'gene'}, use_global_device_ids=true, to_apply=%region_16.0 | all-reduce | flops 4096 | bytes 32768 | tf_op jit(solution)/shard_map/psum | solution.py:44
  583.6 6.4 collective-permute-done.9
  590.0 7.5 collective-permute-done.10
  597.7 9.0 collective-permute-done.11
  609.1 29.6 %all-reduce.16.cloned.1.call-done = bf16[64,2560]{1,0:T(8,128)(2,1)} async-done(((bf16[64,2560]{1,0:T(8,128)(2,1)}), bf16[64,2560]{1,0:T(8,128)(2,1)}) %all-reduce.16.cloned.1.call-update) | async-done | bytes 327696 | tf_op jit(solution)/shard_map/psum | solution.py:41
  640.7 37.1 %psum.158 = f32[64,64]{0,1:T(8,128)S(1)} all-reduce(f32[64,64]{0,1:T(8,128)S(1)} %fusion.122), channel_id=1, replica_groups=mesh['gene'=8,'cell'=4] {'gene'}, use_global_device_ids=true, to_apply=%region_21.0 | all-reduce | flops 4096 | bytes 32768 | tf_op jit(solution)/shard_map/psum | solution.py:44
  696.5 6.4 collective-permute-done.12
  703.0 7.5 collective-permute-done.13
  710.6 9.0 collective-permute-done.14
  721.8 29.8 %all-reduce.18.cloned.1.call-done = bf16[64,2560]{1,0:T(8,128)(2,1)} async-done(((bf16[64,2560]{1,0:T(8,128)(2,1)}), bf16[64,2560]{1,0:T(8,128)(2,1)}) %all-reduce.18.cloned.1.call-update) | async-done | bytes 327696 | tf_op jit(solution)/shard_map/psum | solution.py:41
  753.5 37.1 %psum.161 = f32[64,64]{0,1:T(8,128)S(1)} all-reduce(f32[64,64]{0,1:T(8,128)S(1)} %fusion.124), channel_id=1, replica_groups=mesh['gene'=8,'cell'=4] {'gene'}, use_global_device_ids=true, to_apply=%region_26.0 | all-reduce | flops 4096 | bytes 32768 | tf_op jit(solution)/shard_map/psum | solution.py:44
  790.7 5.8 cholesky.163
  809.2 6.4 collective-permute-done.15
  815.7 7.5 collective-permute-done.16
  823.3 9.0 collective-permute-done.17
  837.1 29.9 %all-reduce.20.cloned.1.call-done = bf16[64,2560]{1,0:T(8,128)(2,1)} async-done(((bf16[64,2560]{1,0:T(8,128)(2,1)}), bf16[64,2560]{1,0:T(8,128)(2,1)}) %all-reduce.20.cloned.1.call-update) | async-done | bytes 327696 | tf_op jit(solution)/shard_map/psum | solution.py:41
  868.8 37.5 %psum.164 = f32[64,64]{0,1:T(8,128)S(1)} all-reduce(f32[64,64]{0,1:T(8,128)S(1)} %fusion.126), channel_id=1, replica_groups=mesh['gene'=8,'cell'=4] {'gene'}, use_global_device_ids=true, to_apply=%region_31.0 | all-reduce | flops 4096 | bytes 32768 | tf_op jit(solution)/shard_map/psum | solution.py:44
  925.0 6.4 collective-permute-done.18
  931.5 7.5 collective-permute-done.19
  939.1 9.0 collective-permute-done.20
  950.3 29.9 %all-reduce.22.cloned.1.call-done = bf16[64,2560]{1,0:T(8,128)(2,1)} async-done(((bf16[64,2560]{1,0:T(8,128)(2,1)}), bf16[64,2560]{1,0:T(8,128)(2,1)}) %all-reduce.22.cloned.1.call-update) | async-done | bytes 327696 | tf_op jit(solution)/shard_map/psum | solution.py:41
  982.0 37.1 %psum.167 = f32[64,64]{0,1:T(8,128)S(1)} all-reduce(f32[64,64]{0,1:T(8,128)S(1)} %fusion.127), channel_id=1, replica_groups=mesh['gene'=8,'cell'=4] {'gene'}, use_global_device_ids=true, to_apply=%region_36.40 | all-reduce | flops 4096 | bytes 32768 | tf_op jit(solution)/shard_map/psum | solution.py:44
  (230 shorter events, 167.7 us)
Async XLA Ops:
  6.5 222.6 %all-reduce.24.cloned.1.call-start = ((), (), s32[]{:S(2)}) async-start(), calls=%async_computation.7 | async-start | bytes 172032 | tf_op jit(solution)/shard_map/psum | solution.py:29
  174.8 11.6 %slice-start.2 = ((s8[5242880]{0:T(1024)(128)(4,1)}), s8[1048576]{0:T(1024)(128)(4,1)S(1)}, s32[]{:S(2)}) async-start(s8[5242880]{0:T(1024)(128)(4,1)} %bitcast.202), calls=%async_computation.10 | async-start | bytes 2097152
  179.0 12.7 %slice-start.8 = ((s8[5242880]{0:T(1024)(128)(4,1)}), s8[4194304]{0:T(1024)(128)(4,1)S(1)}, s32[]{:S(2)}) async-start(s8[5242880]{0:T(1024)(128)(4,1)} %bitcast.208), calls=%async_computation.16 | async-start | bytes 8388608
  179.0 12.7 %slice-start.12 = ((s8[5242880]{0:T(1024)(128)(4,1)}), s8[4194304]{0:T(1024)(128)(4,1)S(1)}, s32[]{:S(2)}) async-start(s8[5242880]{0:T(1024)(128)(4,1)} %bitcast.212), calls=%async_computation.20 | async-start | bytes 8388608
  191.8 38.0 %copy-start = (f32[64,2560]{1,0:T(8,128)S(1)}, f32[64,2560]{1,0:T(8,128)}, u32[]{:S(2)}) copy-start(f32[64,2560]{1,0:T(8,128)} %param.10) | copy-start | bytes 1966084
  195.5 104.0 %all-reduce.10.cloned.1.call-start = ((), (), s32[]{:S(2)}) async-start(), calls=%async_computation | async-start | bytes 655360 | tf_op jit(solution)/shard_map/psum | solution.py:41
  229.8 34.8 %slice-start.16 = ((s8[5242880]{0:T(1024)(128)(4,1)}), s8[4194304]{0:T(1024)(128)(4,1)S(1)}, s32[]{:S(2)}) async-start(s8[5242880]{0:T(1024)(128)(4,1)} %bitcast.216), calls=%async_computation.24 | async-start | bytes 8388608
  230.2 34.5 %slice-start.17 = ((s8[5242880]{0:T(1024)(128)(4,1)}), s8[1048576]{0:T(1024)(128)(4,1)S(1)}, s32[]{:S(2)}) async-start(s8[5242880]{0:T(1024)(128)(4,1)} %bitcast.216), calls=%async_computation.25 | async-start | bytes 2097152
  234.7 8.5 collective-permute-start
  243.2 7.8 collective-permute-start.1
  251.1 15.6 %copy-start.6 = (f32[2560]{0:T(1024)S(1)}, f32[2560]{0:T(1024)}, u32[]{:S(2)}) copy-start(f32[2560]{0:T(1024)} %get-tuple-element.8) | copy-start | bytes 30724
  251.1 13.4 %collective-permute-start.2 = (f32[64,1024]{1,0:T(8,128)S(1)}, f32[64,1024]{1,0:T(8,128)S(1)}, u32[]{:S(2)}, u32[]{:S(2)}) collective-permute-start(f32[64,1024]{1,0:T(8,128)S(1)} %add.141), channel_id=1, source_target_pairs={{0,16},{4,20},{8,24},{12,28},{16,0},{20,4},{24,8},{28,12},{1,17},{... | collective-permute-start | bytes 786440 | tf_op jit(solution)/shard_map/ppermute | solution.py:36
  266.6 145.9 %all-reduce.12.cloned.1.call-start = ((), (), s32[]{:S(2)}) async-start(), calls=%async_computation.1 | async-start | bytes 655360 | tf_op jit(solution)/shard_map/psum | solution.py:41
  350.6 30.0 %slice-start.14 = ((s8[5242880]{0:T(1024)(128)(4,1)}), s8[4194304]{0:T(1024)(128)(4,1)S(1)}, s32[]{:S(2)}) async-start(s8[5242880]{0:T(1024)(128)(4,1)} %bitcast.214), calls=%async_computation.22 | async-start | bytes 8388608
  352.9 27.8 %slice-start.15 = ((s8[5242880]{0:T(1024)(128)(4,1)}), s8[1048576]{0:T(1024)(128)(4,1)S(1)}, s32[]{:S(2)}) async-start(s8[5242880]{0:T(1024)(128)(4,1)} %bitcast.214), calls=%async_computation.23 | async-start | bytes 2097152
  357.2 6.4 collective-permute-start.3
  363.7 7.6 collective-permute-start.4
  371.4 9.1 collective-permute-start.5
  382.6 143.2 %all-reduce.14.cloned.1.call-start = ((), (), s32[]{:S(2)}) async-start(), calls=%async_computation.2 | async-start | bytes 655360 | tf_op jit(solution)/shard_map/psum | solution.py:41
  463.9 30.0 %slice-start.10 = ((s8[5242880]{0:T(1024)(128)(4,1)}), s8[4194304]{0:T(1024)(128)(4,1)S(1)}, s32[]{:S(2)}) async-start(s8[5242880]{0:T(1024)(128)(4,1)} %bitcast.210), calls=%async_computation.18 | async-start | bytes 8388608
  466.1 27.8 %slice-start.11 = ((s8[5242880]{0:T(1024)(128)(4,1)}), s8[1048576]{0:T(1024)(128)(4,1)S(1)}, s32[]{:S(2)}) async-start(s8[5242880]{0:T(1024)(128)(4,1)} %bitcast.210), calls=%async_computation.19 | async-start | bytes 2097152
  470.5 6.4 collective-permute-start.6
  476.9 7.6 collective-permute-start.7
  484.6 9.1 collective-permute-start.8
  495.8 143.0 %all-reduce.16.cloned.1.call-start = ((), (), s32[]{:S(2)}) async-start(), calls=%async_computation.3 | async-start | bytes 655360 | tf_op jit(solution)/shard_map/psum | solution.py:41
  527.6 79.3 %slice-start.6 = ((s8[5242880]{0:T(1024)(128)(4,1)}), s8[1048576]{0:T(1024)(128)(4,1)S(1)}, s32[]{:S(2)}) async-start(s8[5242880]{0:T(1024)(128)(4,1)} %bitcast.206), calls=%async_computation.14 | async-start | bytes 2097152
  579.0 27.8 %slice-start.7 = ((s8[5242880]{0:T(1024)(128)(4,1)}), s8[4194304]{0:T(1024)(128)(4,1)S(1)}, s32[]{:S(2)}) async-start(s8[5242880]{0:T(1024)(128)(4,1)} %bitcast.206), calls=%async_computation.15 | async-start | bytes 8388608
  583.5 6.4 collective-permute-start.9
  590.0 7.6 collective-permute-start.10
  597.6 11.5 %copy-start.3 = (f32[2560]{0:T(1024)S(1)}, f32[2560]{0:T(1024)}, u32[]{:S(2)}) copy-start(f32[2560]{0:T(1024)} %get-tuple-element.12) | copy-start | bytes 30724
  597.6 9.1 collective-permute-start.11
  608.8 142.9 %all-reduce.18.cloned.1.call-start = ((), (), s32[]{:S(2)}) async-start(), calls=%async_computation.4 | async-start | bytes 655360 | tf_op jit(solution)/shard_map/psum | solution.py:41
  638.8 81.0 %slice-start.4 = ((s8[5242880]{0:T(1024)(128)(4,1)}), s8[1048576]{0:T(1024)(128)(4,1)S(1)}, s32[]{:S(2)}) async-start(s8[5242880]{0:T(1024)(128)(4,1)} %bitcast.204), calls=%async_computation.12 | async-start | bytes 2097152
  692.0 27.8 %slice-start.5 = ((s8[5242880]{0:T(1024)(128)(4,1)}), s8[4194304]{0:T(1024)(128)(4,1)S(1)}, s32[]{:S(2)}) async-start(s8[5242880]{0:T(1024)(128)(4,1)} %bitcast.204), calls=%async_computation.13 | async-start | bytes 8388608
  696.4 6.4 collective-permute-start.12
  702.9 7.6 collective-permute-start.13
  710.6 9.1 collective-permute-start.14
  721.8 145.2 %all-reduce.20.cloned.1.call-start = ((), (), s32[]{:S(2)}) async-start(), calls=%async_computation.5 | async-start | bytes 655360 | tf_op jit(solution)/shard_map/psum | solution.py:41
  809.1 6.4 collective-permute-start.15
  815.6 7.6 collective-permute-start.16
  823.2 13.8 %copy-start.1 = (f32[2560]{0:T(1024)S(1)}, f32[2560]{0:T(1024)}, u32[]{:S(2)}) copy-start(f32[2560]{0:T(1024)} %get-tuple-element.14) | copy-start | bytes 30724
  823.3 9.1 collective-permute-start.17
  832.5 115.8 %slice-start = ((s8[5242880]{0:T(1024)(128)(4,1)}), s8[1048576]{0:T(1024)(128)(4,1)S(1)}, s32[]{:S(2)}) async-start(s8[5242880]{0:T(1024)(128)(4,1)} %bitcast.200), calls=%async_computation.8 | async-start | bytes 2097152
  837.0 143.2 %all-reduce.22.cloned.1.call-start = ((), (), s32[]{:S(2)}) async-start(), calls=%async_computation.6 | async-start | bytes 655360 | tf_op jit(solution)/shard_map/psum | solution.py:41
  918.4 29.9 %slice-start.1 = ((s8[5242880]{0:T(1024)(128)(4,1)}), s8[4194304]{0:T(1024)(128)(4,1)S(1)}, s32[]{:S(2)}) async-start(s8[5242880]{0:T(1024)(128)(4,1)} %bitcast.200), calls=%async_computation.9 | async-start | bytes 8388608
  924.9 6.4 collective-permute-start.18
  931.4 7.6 collective-permute-start.19
  939.1 9.1 collective-permute-start.20
  (6 other events, 52.0 us)
Sparse Core Ops, SparseCore 0:
  195.6 33.3 all-reduce.23
  266.8 32.7 all-reduce.9
  382.7 29.7 all-reduce.11
  495.9 29.7 all-reduce.13
  608.9 29.7 all-reduce.15
  721.9 29.7 all-reduce.17
  837.1 29.7 all-reduce.19
  950.4 29.7 all-reduce.21
